TPU v7x, 32 devices: a whole 2x2x4 slice. The times are simulated.
32 devices in a mesh: blk: 8 (over z, x), span: 4 (over y, core).
Axes of the slice: x: 2, y: 2, z: 4, core: 2. Of those that a mesh axis runs over, the one named last changes fastest.
Arguments:
- fields: float32 [5, 125, 16384], P(None, None, ('blk', 'span')), may hold values from -6 to 6
- section_store: float32 [5, 125, 16384], P(None, None, ('blk', 'span')), may hold values from -6 to 6
- mean_velocity: float32 [3, 125, 16384], P(None, None, ('blk', 'span')), may hold values from -0.6 to 0.6
- sound_speed: float32 [125, 16384], P(None, ('blk', 'span')), may hold values from 0.7 to 1.5
- element_slot: int32 [16384], P(('blk', 'span')), may hold values from 0 to 511, as said below
- face_turn: int32 [8, 16], P('blk', 'span'), may hold values from 0 to 7
- rotor_offset: int32 [16], P('span'), may hold values from 0 to 7
Outputs:
- fields_next: float32 [5, 125, 16384], P(None, None, ('blk', 'span'))
- store_next: float32 [5, 125, 16384], P(None, None, ('blk', 'span'))
Inputs may be any that keep to these rules, and one draw needn't show every extreme that they name: `element_slot`: in each aligned block of 512 entries (the elements of one device) every number 0 to 511 appears once.
All inputs are finite; a program needn't handle non-finite values.
Results may differ from a plain program's by a relative error of at most 0.0003.
Values sent between devices are 32-bit elements; how exact they have to be, the bound alone decides.
A program may use at most 128 MiB of HBM per device.

v0:
```python
import functools

import jax
import jax.numpy as jnp
import numpy as np
from jax import lax
from jax.experimental import pallas as pl
from jax.experimental.pallas import tpu as pltpu
from jax.sharding import PartitionSpec as P

ORDER = 4
N1 = ORDER + 1
FACE = N1 * N1
NODES = N1**3
ROWS = 128
OFF = 32
FROWS = 32
EARLY = 88
SENT = ((0, 1, 2, 3, 4, 5, 8), (0, 1, 2, 3, 4, 6, 8), (0, 1, 2, 3, 4, 7, 8))

section_decay = -567301805773.0 / 1357537059087.0
section_gain = 5161836677717.0 / 13612068292357.0
time_step = 0.05
metric_scale = (1.0, 1.5, 0.75)
end_weight = 0.1
MESH = pl.DeviceIdType.MESH
F32 = jnp.float32
BF16 = jnp.bfloat16


def lobatto_slopes():
    r = np.sqrt(3.0 / 7.0)
    x = np.array([-1.0, -r, 0.0, r, 1.0])
    n = x.shape[0]
    d = np.zeros((n, n))
    for i in range(n):
        for j in range(n):
            if i == j:
                d[i, j] = sum(1.0 / (x[i] - x[m]) for m in range(n) if m != i)
            else:
                a = np.prod([x[i] - x[m] for m in range(n) if m != i])
                b = np.prod([x[j] - x[m] for m in range(n) if m != j])
                d[i, j] = a / (b * (x[i] - x[j]))
    return d


def derivative_tables():
    slopes = lobatto_slopes().astype(np.float32).astype(np.float64)
    eye = np.eye(N1)
    full = np.zeros((ROWS, 3 * ROWS))
    for d in range(3):
        mats = [eye, eye, eye]
        mats[d] = slopes
        big = np.kron(np.kron(mats[0], mats[1]), mats[2])
        full[:NODES, d * ROWS : d * ROWS + NODES] = -metric_scale[d] * big
    hi = np.asarray(full, np.float32).astype(jnp.bfloat16)
    lo = (full - hi.astype(np.float64)).astype(np.float32).astype(jnp.bfloat16)
    return np.concatenate([hi, hi], axis=1), lo


def turn_tables():
    base = np.arange(FACE).reshape(N1, N1)
    pick = np.zeros((9 * FROWS, ROWS), np.float32)
    place = np.zeros((9 * ROWS, FROWS), np.float32)
    for n in range(FACE):
        pick[n, N1 * n + N1 - 1] = 1
        place[N1 * n + N1 - 1, n] = 1
    for o in range(8):
        fwd = base.T if o & 4 else base
        fwd = fwd[::-1] if o & 1 else fwd
        fwd = fwd[:, ::-1] if o & 2 else fwd
        inv = base[:, ::-1] if o & 2 else base
        inv = inv[::-1] if o & 1 else inv
        inv = inv.T if o & 4 else inv
        for n in range(FACE):
            pick[(o + 1) * FROWS + n, N1 * inv.reshape(-1)[n]] = 1
            place[(o + 1) * ROWS + N1 * n, fwd.reshape(-1)[n]] = 1
    return pick.astype(jnp.bfloat16), place.astype(jnp.bfloat16)


def split(x):
    hi = x.astype(BF16)
    return hi, (x - hi.astype(F32)).astype(BF16)


def dot(a, b):
    return jnp.dot(a, b, preferred_element_type=F32)


def dot_t(a, b):
    return lax.dot_general(a, b, (((1,), (1,)), ((), ())), preferred_element_type=F32)


def flux(state, d):
    q, m, c = state[:5], state[5], state[6]
    cu, cp = c * q[1 + d], c * q[4]
    out = [m * v for v in q]
    out[0] = out[0] + cu
    out[1 + d] = out[1 + d] + cp
    out[4] = out[4] + cu
    return out


def correction(own, outer, sign, d):
    w = 0.5 * metric_scale[d] / end_weight
    reach = jnp.maximum(jnp.abs(own[5]) + own[6], jnp.abs(outer[5]) + outer[6])
    fo, fx = flux(own, d), flux(outer, d)
    return [w * (sign * (fo[k] - fx[k]) + reach * (outer[k] - own[k])) for k in range(5)]


def kernel(
    n_blk, n_span, per_span, axial, fields_in, mean_in, sound_in, slot, turns, offs, w_hi_in, w_lo_in,
    pick_in, place_in,
    out, e, perm, fb, rates, th_send, th_recv, th_out, far_slot, cross, sp_send, sp_recv, sp_rows, pk,
    gath, iface, fields, mean, sound, w_hi, w_lo, pick, place,
    th_ss, th_rs, sp_ss, sp_rs, if_ss, if_rs, loaded,
):
    elems = per_span * axial
    half = axial // 2
    blk, slab = lax.axis_index("blk"), lax.axis_index("span")
    up, down = lax.rem(blk + 1, n_blk), lax.rem(blk + n_blk - 1, n_blk)
    right, left = lax.rem(slab + 1, n_span), lax.rem(slab + n_span - 1, n_span)

    first = pl.ds(0, 1)
    pairs = (
        (fields_in, fields), (mean_in.at[first], mean.at[first]), (sound_in, sound),
        (mean_in.at[pl.ds(1, 2)], mean.at[pl.ds(1, 2)]), (w_hi_in, w_hi), (w_lo_in, w_lo),
        (pick_in, pick), (place_in, place),
    )
    loads = [pltpu.make_async_copy(a, b, loaded.at[n]) for n, (a, b) in enumerate(pairs)]
    for load in loads:
        load.start()
    barrier = pltpu.get_barrier_semaphore()
    for k in range(1, n_blk):
        pl.semaphore_signal(
            barrier, inc=1, device_id={"blk": lax.rem(blk + k, n_blk)}, device_id_type=MESH
        )
    for side in (right, left):
        pl.semaphore_signal(barrier, inc=1, device_id={"span": side}, device_id_type=MESH)

    last = NODES - FACE
    theta_own = [fields.at[k] for k in range(5)] + [mean.at[0], sound]
    for load in loads[:3]:
        load.wait()
    for n, ref in enumerate(theta_own):
        th_send[0, n * FACE : (n + 1) * FACE] = ref[last:NODES]
        th_send[1, n * FACE : (n + 1) * FACE] = ref[:FACE]

    def start(src, dst, ss, rs, target):
        copy = pltpu.make_async_remote_copy(
            src_ref=src, dst_ref=dst, send_sem=ss, recv_sem=rs, device_id=target,
            device_id_type=MESH,
        )
        copy.start()
        return copy

    pl.semaphore_wait(barrier, n_blk + 1)
    slot_up = start(slot, far_slot.at[0], th_ss.at[2], th_rs.at[2], {"blk": up})
    slot_dn = start(slot, far_slot.at[1], th_ss.at[3], th_rs.at[3], {"blk": down})
    th_up = start(th_send.at[0], th_recv.at[0], th_ss.at[0], th_rs.at[0], {"blk": up})
    th_dn = start(
        th_send.at[1, :EARLY], th_recv.at[1, :EARLY], th_ss.at[1], th_rs.at[1], {"blk": down}
    )

    rows_i = lax.broadcasted_iota(jnp.int32, (elems, elems), 0)
    perm[...] = jnp.where(rows_i == slot[...], 1.0, 0.0).astype(BF16)

    def gather(f, value):
        hi, lo = split(value)
        e[f, :OFF] = jnp.zeros((OFF, elems), F32)
        e[f, OFF + 120 :] = jnp.zeros((e.shape[1] - OFF - 120, elems), F32)
        e[f, OFF : OFF + NODES] = dot(hi, perm[...]) + dot(lo, perm[...])

    for f in range(5):
        gather(f, fields[f])
    for load in loads[3:]:
        load.wait()
    for d in range(3):
        gather(5 + d, mean[d])
    gather(8, sound[...])

    cells = 2 * per_span
    col = lax.broadcasted_iota(jnp.int32, (elems, 128), 1)
    cell = lax.rem(col, cells)
    first_lane = lax.rem(cell, per_span) * axial + half
    elem = lax.broadcasted_iota(jnp.int32, (elems, 128), 0)
    own_side = jnp.where(elem == first_lane - 1 + cell // per_span, 1.0, 0.0).astype(BF16)
    far_side = jnp.where(elem == first_lane - cell // per_span, 1.0, 0.0).astype(BF16)
    lane = lax.broadcasted_iota(jnp.int32, (1, 128), 1)
    lane_f, lane_cell = lane // cells, lax.rem(lane, cells)
    lane_s = lax.rem(lane_cell, per_span)
    stator = lane_cell < per_span
    code = jnp.zeros((1, 128), jnp.int32)
    turn_by = jnp.zeros((1, 128), jnp.int32)
    for s in range(per_span):
        code = jnp.where(lane_s == s, turns[0, s], code)
        turn_by = jnp.where(lane_s == s, offs[s], turn_by)
    block = slice(OFF, OFF + ROWS)
    z = jnp.zeros((ROWS, 128), F32)
    for n, f in enumerate(SENT[2]):
        hi, lo = split(e[f, block])
        z = jnp.where(lane_f == n, dot(hi, own_side) + dot(lo, own_side), z)
    hi, lo = split(z)
    picked = dot(pick[...], hi) + dot(pick[...], lo)
    packet = picked[:FROWS]
    for o in range(8):
        part = picked[(o + 1) * FROWS : (o + 2) * FROWS]
        packet = jnp.where(jnp.logical_and(jnp.logical_not(stator), code == o), part, packet)
    half_rows = FROWS // 2
    pk[...] = jnp.where(lane < 64, packet[:half_rows], pltpu.roll(packet[half_rows:], 64, 1))
    for n, f in enumerate(SENT[1]):
        for i in range(N1):
            at = OFF + i * FACE
            sp_send[0, n, i * N1 : (i + 1) * N1] = e[f, at + 20 : at + 25, elems - axial :]
            sp_send[1, n, i * N1 : (i + 1) * N1] = e[f, at : at + 5, :axial]
    if_copies = [
        start(pk, gath.at[k - 1], if_ss.at[k - 1], if_rs.at[k - 1], {"blk": lax.rem(blk + k, n_blk)})
        for k in range(1, n_blk)
    ]
    sp_up = start(sp_send.at[0], sp_recv.at[0], sp_ss.at[0], sp_rs.at[0], {"span": right})
    sp_dn = start(sp_send.at[1], sp_recv.at[1], sp_ss.at[1], sp_rs.at[1], {"span": left})
    th_rest = start(
        th_send.at[1, EARLY:], th_recv.at[1, EARLY:], th_ss.at[4], th_rs.at[4], {"blk": down}
    )

    for s in range(per_span):
        ln = slice(s * axial, (s + 1) * axial)
        for d in range(3):
            for k, v in enumerate(flux([e[f, block, ln] for f in SENT[d]], d)):
                hi, lo = split(v)
                at = slice(k * elems + s * axial, k * elems + (s + 1) * axial)
                fb[d * ROWS : (d + 1) * ROWS, at] = hi
                fb[(3 + d) * ROWS : (4 + d) * ROWS, at] = lo
    for k in range(5):
        at = slice(k * elems, (k + 1) * elems)
        rates[k] = dot(w_hi[...], fb[:, at]) + dot(w_lo[...], fb[: 3 * ROWS, at])

    for side, copy in enumerate((slot_up, slot_dn)):
        copy.wait()
        far = jnp.where(rows_i == far_slot[side], 1.0, 0.0).astype(BF16)
        cross[side] = dot_t(far, perm[...]).astype(BF16)

    row = lax.broadcasted_iota(jnp.int32, (ROWS, axial), 0)
    a_id = lax.broadcasted_iota(jnp.int32, (ROWS, axial), 1)
    k_id = lax.rem(row // N1, N1)
    sp_up.wait()
    sp_dn.wait()
    for n in range(7):
        for i in range(N1):
            at = i * FACE
            sp_rows[n, at : at + 5] = sp_recv[0, n, i * N1 : (i + 1) * N1]
            sp_rows[n, at + 20 : at + 25] = sp_recv[1, n, i * N1 : (i + 1) * N1]
    low = k_id == 0
    face = jnp.logical_and(jnp.logical_or(low, k_id == N1 - 1), row < NODES)
    sign = jnp.where(low, -1.0, 1.0)
    for s in range(per_span):
        ln = slice(s * axial, (s + 1) * axial)
        own = [e[f, block, ln] for f in SENT[1]]
        outer = []
        for n, f in enumerate(SENT[1]):
            wall = -own[n] if n == 2 else own[n]
            if s == 0:
                lo_v = jnp.where(slab > 0, sp_rows[n], wall)
            else:
                lo_v = e[f, OFF + 20 : OFF + 20 + ROWS, (s - 1) * axial : s * axial]
            if s == per_span - 1:
                hi_v = jnp.where(slab < n_span - 1, sp_rows[n], wall)
            else:
                hi_v = e[f, OFF - 20 : OFF - 20 + ROWS, (s + 1) * axial : (s + 2) * axial]
            outer.append(jnp.where(low, lo_v, hi_v))
        for k, v in enumerate(correction(own, outer, sign, 1)):
            rates[k, :, ln] += jnp.where(face, v, 0.0)

    for copy in if_copies:
        copy.wait()
    steps = jnp.where(stator, turn_by, lax.rem(n_blk - turn_by, n_blk))
    chosen = pk[...]
    for k in range(1, n_blk):
        chosen = jnp.where(steps == k, gath[k - 1], chosen)
    hi, lo = split(jnp.concatenate([chosen, pltpu.roll(chosen, 64, 1)], axis=0))
    placed = dot(place[...], hi) + dot(place[...], lo)
    turned = placed[:ROWS]
    for o in range(8):
        part = placed[(o + 1) * ROWS : (o + 2) * ROWS]
        turned = jnp.where(jnp.logical_and(stator, code == o), part, turned)
    for n in range(7):
        hi, lo = split(jnp.where(lane_f == n, turned, 0.0))
        iface[n] = dot_t(hi, far_side) + dot_t(lo, far_side)

    l_id = lax.rem(row, N1)
    low = l_id == 0
    face = jnp.logical_and(jnp.logical_or(low, l_id == N1 - 1), row < NODES)
    sign = jnp.where(low, -1.0, 1.0)
    slides = a_id == jnp.where(low, half, half - 1)
    ends = a_id == jnp.where(low, 0, axial - 1)
    for s in range(per_span):
        ln = slice(s * axial, (s + 1) * axial)
        own = [e[f, block, ln] for f in SENT[2]]
        outer = []
        for n, f in enumerate(SENT[2]):
            lo_v = pltpu.roll(e[f, OFF + 4 : OFF + 4 + ROWS, ln], 1, 1)
            hi_v = pltpu.roll(e[f, OFF - 4 : OFF - 4 + ROWS, ln], axial - 1, 1)
            v = jnp.where(slides, iface[n, :, ln], jnp.where(low, lo_v, hi_v))
            outer.append(jnp.where(ends, own[n] if n > 4 else 0.0, v))
        for k, v in enumerate(correction(own, outer, sign, 2)):
            rates[k, :, ln] += jnp.where(face, v, 0.0)

    for k in range(5):
        hi, lo = split(rates[k])
        out[k] = (dot_t(hi, perm[...]) + dot_t(lo, perm[...]))[:NODES]

    def theta(side, first, sgn):
        hi, lo = split(th_recv[side, : 7 * FACE])
        th_out[: 7 * FACE] = dot(hi, cross[side]) + dot(lo, cross[side])
        own = [ref[first : first + FACE] for ref in theta_own]
        outer = [th_out[n * FACE : (n + 1) * FACE] for n in range(7)]
        for k, v in enumerate(correction(own, outer, sgn, 0)):
            out[k, first : first + FACE] += v

    th_up.wait()
    theta(0, 0, -1.0)
    th_dn.wait()
    th_rest.wait()
    theta(1, last, 1.0)


def on_device(fields, store, mean, sound, slot, turns, offs, n_blk, n_span):
    per_theta, per_span = turns.shape
    assert per_theta == 1
    elems = slot.shape[0]
    axial = elems // per_span
    w_hi, w_lo = (jnp.asarray(t) for t in derivative_tables())
    pick, place = (jnp.asarray(t) for t in turn_tables())
    vmem = pl.BlockSpec(memory_space=pltpu.VMEM)
    hbm = pl.BlockSpec(memory_space=pl.ANY)
    smem = pl.BlockSpec(memory_space=pltpu.SMEM)
    dma = pltpu.SemaphoreType.DMA
    stored = pl.pallas_call(
        functools.partial(kernel, n_blk, n_span, per_span, axial),
        out_shape=jax.ShapeDtypeStruct((5, NODES, elems), F32),
        in_specs=[hbm] * 3 + [vmem] + [smem] * 2 + [hbm] * 4,
        out_specs=vmem,
        scratch_shapes=[
            pltpu.VMEM((9, OFF + ROWS + 32, elems), F32),
            pltpu.VMEM((elems, elems), BF16),
            pltpu.VMEM((6 * ROWS, 5 * elems), BF16),
            pltpu.VMEM((5, ROWS, elems), F32),
            pltpu.VMEM((2, 7 * FACE + 1, elems), F32),
            pltpu.VMEM((2, 7 * FACE + 1, elems), F32),
            pltpu.VMEM((7 * FACE + 1, elems), F32),
            pltpu.VMEM((2, 1, elems), jnp.int32),
            pltpu.VMEM((2, elems, elems), BF16),
            pltpu.VMEM((2, 7, FROWS, axial), F32),
            pltpu.VMEM((2, 7, FROWS, axial), F32),
            pltpu.VMEM((7, ROWS, axial), F32),
            pltpu.VMEM((FROWS // 2, 128), F32),
            pltpu.VMEM((n_blk - 1, FROWS // 2, 128), F32),
            pltpu.VMEM((7, ROWS, elems), F32),
            pltpu.VMEM(fields.shape, F32),
            pltpu.VMEM(mean.shape, F32),
            pltpu.VMEM(sound.shape, F32),
            *(pltpu.VMEM(t.shape, BF16) for t in (w_hi, w_lo, pick, place)),
            dma((5,)), dma((5,)), dma((2,)), dma((2,)), dma((n_blk - 1,)), dma((n_blk - 1,)),
            dma((8,)),
        ],
        compiler_params=pltpu.CompilerParams(collective_id=0, has_side_effects=True),
    )(fields, mean, sound, slot.reshape(1, elems), turns, offs, w_hi, w_lo, pick, place)
    store_next = section_decay * store + time_step * stored
    return fields + section_gain * store_next, store_next


def solution(mesh):
    whole = P(None, None, ("blk", "span"))
    in_specs = (
        whole, whole, whole, P(None, ("blk", "span")), P(("blk", "span")), P("blk", "span"), P("span"),
    )
    body = functools.partial(on_device, n_blk=mesh.shape["blk"], n_span=mesh.shape["span"])
    return jax.shard_map(
        body, mesh=mesh, in_specs=in_specs, out_specs=(whole, whole), check_vma=False
    )
```

profile of v0, /device:TPU:0, one launch (start us, length us, event | category | flops | bytes accessed | tf_op | source)
XLA Modules:
  0.0 33.5 jit_solution(7858526500660040351)
XLA Ops:
  0.6 0.0 copy-start
  0.6 0.0 copy-start.1
  0.7 29.6 %shard_map.122 = f32[5,125,512]{2,1,0:T(8,128)} custom-call(f32[5,125,512]{2,1,0:T(8,128)} %fields_in.1, f32[3,125,512]{2,1,0:T(8,128)} %mean_in.1, f32[125,512]{1,0:T(8,128)} %sound_in.1, s32[1,512]{1,0:T(1,128)} %bitcast.1, s32[1,4]{1,0:T(1,128)} %turns.1, s32[4]{0:T(128)} %offs.1, bf16[128,768]{1,0:T(8,128)(2,1)} %constant.14.clone.w_hi_in, ...), custom_call_target="tpu_custom_call" | custom-call | tf_op jit(solution)/shard_map/pallas_call | solution.py:338
  30.2 0.0 copy-done
  30.2 0.0 copy-done.1
  30.2 3.3 %multiply_add_fusion = (f32[5,125,512]{2,1,0:T(8,128)}, f32[5,125,512]{2,1,0:T(8,128)}) fusion(f32[5,125,512]{2,1,0:T(8,128)S(1)} %copy-done, f32[5,125,512]{2,1,0:T(8,128)} %shard_map.122, f32[5,125,512]{2,1,0:T(8,128)S(1)} %copy-done.1), kind=kLoop, calls=%fused_computation | loop fusion | flops 1600000 | bytes 6400000 | tf_op jit(solution)/shard_map/add | solution.py:369
Async XLA Ops:
  0.6 29.6 %copy-start = (f32[5,125,512]{2,1,0:T(8,128)S(1)}, f32[5,125,512]{2,1,0:T(8,128)}, u32[]{:S(2)}) copy-start(f32[5,125,512]{2,1,0:T(8,128)} %fields_in.1) | copy-start | bytes 3840004
  0.6 29.6 %copy-start.1 = (f32[5,125,512]{2,1,0:T(8,128)S(1)}, f32[5,125,512]{2,1,0:T(8,128)}, u32[]{:S(2)}) copy-start(f32[5,125,512]{2,1,0:T(8,128)} %param.12) | copy-start | bytes 3840004
where the time goes:
time: 33.7 us; the launch traced here: 33.5 us
  Pallas kernels  29.6 us (88%)
  other arithmetic  3.29 us (10%)
  between operations  0.67 us (2%)
    pallas_call x1, Pallas kernels, on_device(): pl.pallas_call(functools.partial(kernel, n_blk, n_span, per_span, axial),...  29.6 us
    add x1, other arithmetic, on_device(): return (fields + section_gain * store_next, store_next)  3.29 us

commit v1 on v0

--- a/solution.py
+++ b/solution.py
@@ -15,7 +15,7 @@
 ROWS = 128
 OFF = 32
 FROWS = 32
-EARLY = 88
+GROUPS = ((0, 8), (8, 16), (16, 25))
 SENT = ((0, 1, 2, 3, 4, 5, 8), (0, 1, 2, 3, 4, 6, 8), (0, 1, 2, 3, 4, 7, 8))
 
 section_decay = -567301805773.0 / 1357537059087.0
@@ -61,10 +61,12 @@
 def turn_tables():
     base = np.arange(FACE).reshape(N1, N1)
     pick = np.zeros((9 * FROWS, ROWS), np.float32)
-    place = np.zeros((9 * ROWS, FROWS), np.float32)
+    turn = np.zeros((8 * FROWS, FROWS), np.float32)
+    put = np.zeros((ROWS, 2 * FROWS), np.float32)
     for n in range(FACE):
         pick[n, N1 * n + N1 - 1] = 1
-        place[N1 * n + N1 - 1, n] = 1
+        put[N1 * n + N1 - 1, n] = 1
+        put[N1 * n, FROWS + n] = 1
     for o in range(8):
         fwd = base.T if o & 4 else base
         fwd = fwd[::-1] if o & 1 else fwd
@@ -74,8 +76,8 @@
         inv = inv.T if o & 4 else inv
         for n in range(FACE):
             pick[(o + 1) * FROWS + n, N1 * inv.reshape(-1)[n]] = 1
-            place[(o + 1) * ROWS + N1 * n, fwd.reshape(-1)[n]] = 1
-    return pick.astype(jnp.bfloat16), place.astype(jnp.bfloat16)
+            turn[o * FROWS + n, fwd.reshape(-1)[n]] = 1
+    return tuple(t.astype(jnp.bfloat16) for t in (pick, turn, put))
 
 
 def split(x):
@@ -110,10 +112,10 @@
 
 def kernel(
     n_blk, n_span, per_span, axial, fields_in, mean_in, sound_in, slot, turns, offs, w_hi_in, w_lo_in,
-    pick_in, place_in,
+    pick_in, turn_in, put_in,
     out, e, perm, fb, rates, th_send, th_recv, th_out, far_slot, cross, sp_send, sp_recv, sp_rows, pk,
-    gath, iface, fields, mean, sound, w_hi, w_lo, pick, place,
-    th_ss, th_rs, sp_ss, sp_rs, if_ss, if_rs, loaded,
+    gath, own_face, slide, fields, mean, sound, w_hi, w_lo, pick, turn, put,
+    th_ss, th_rs, sl_ss, sl_rs, sp_ss, sp_rs, if_ss, if_rs, loaded, ready, near,
 ):
     elems = per_span * axial
     half = axial // 2
@@ -125,16 +127,23 @@
     pairs = (
         (fields_in, fields), (mean_in.at[first], mean.at[first]), (sound_in, sound),
         (mean_in.at[pl.ds(1, 2)], mean.at[pl.ds(1, 2)]), (w_hi_in, w_hi), (w_lo_in, w_lo),
-        (pick_in, pick), (place_in, place),
+        (pick_in, pick), (turn_in, turn), (put_in, put),
     )
     loads = [pltpu.make_async_copy(a, b, loaded.at[n]) for n, (a, b) in enumerate(pairs)]
     for load in loads:
         load.start()
+    even = lax.rem(blk, 2) == 0
+    odd = jnp.logical_not(even)
     barrier = pltpu.get_barrier_semaphore()
+
+    def greet(sem, target, cond):
+        @pl.when(cond)
+        def _():
+            pl.semaphore_signal(sem, inc=1, device_id={"blk": target}, device_id_type=MESH)
+
     for k in range(1, n_blk):
-        pl.semaphore_signal(
-            barrier, inc=1, device_id={"blk": lax.rem(blk + k, n_blk)}, device_id_type=MESH
-        )
+        greet(barrier, lax.rem(blk + k, n_blk), blk + k < n_blk)
+    greet(barrier, down, odd)
     for side in (right, left):
         pl.semaphore_signal(barrier, inc=1, device_id={"span": side}, device_id_type=MESH)
 
@@ -142,50 +151,50 @@
     theta_own = [fields.at[k] for k in range(5)] + [mean.at[0], sound]
     for load in loads[:3]:
         load.wait()
-    for n, ref in enumerate(theta_own):
-        th_send[0, n * FACE : (n + 1) * FACE] = ref[last:NODES]
-        th_send[1, n * FACE : (n + 1) * FACE] = ref[:FACE]
-
-    def start(src, dst, ss, rs, target):
-        copy = pltpu.make_async_remote_copy(
+    for a, b in GROUPS:
+        for n, ref in enumerate(theta_own):
+            at = 7 * a + n * (b - a)
+            th_send[0, at : at + b - a] = ref[last + a : last + b]
+            th_send[1, at : at + b - a] = ref[a:b]
+
+    def remote(src, dst, ss, rs, target):
+        return pltpu.make_async_remote_copy(
             src_ref=src, dst_ref=dst, send_sem=ss, recv_sem=rs, device_id=target,
             device_id_type=MESH,
         )
-        copy.start()
-        return copy
-
-    pl.semaphore_wait(barrier, n_blk + 1)
-    slot_up = start(slot, far_slot.at[0], th_ss.at[2], th_rs.at[2], {"blk": up})
-    slot_dn = start(slot, far_slot.at[1], th_ss.at[3], th_rs.at[3], {"blk": down})
-    th_up = start(th_send.at[0], th_recv.at[0], th_ss.at[0], th_rs.at[0], {"blk": up})
-    th_dn = start(
-        th_send.at[1, :EARLY], th_recv.at[1, :EARLY], th_ss.at[1], th_rs.at[1], {"blk": down}
-    )
-
-    rows_i = lax.broadcasted_iota(jnp.int32, (elems, elems), 0)
-    perm[...] = jnp.where(rows_i == slot[...], 1.0, 0.0).astype(BF16)
-
-    def gather(f, value):
-        hi, lo = split(value)
-        e[f, :OFF] = jnp.zeros((OFF, elems), F32)
-        e[f, OFF + 120 :] = jnp.zeros((e.shape[1] - OFF - 120, elems), F32)
-        e[f, OFF : OFF + NODES] = dot(hi, perm[...]) + dot(lo, perm[...])
-
-    for f in range(5):
-        gather(f, fields[f])
+
+    def flow(side, target):
+        at = [slice(7 * a, 7 * b + (b == FACE)) for a, b in GROUPS]
+        return [
+            remote(th_send.at[side, r], th_recv.at[side, r], th_ss.at[side, g], th_rs.at[side, g], {"blk": target})
+            for g, r in enumerate(at)
+        ]
+
+    ups, dns = flow(0, up), flow(1, down)
+    slots = [
+        remote(slot, far_slot.at[n], sl_ss.at[n], sl_rs.at[n], {"blk": t}) for n, t in enumerate((up, down))
+    ]
+    pl.semaphore_wait(barrier, blk + jnp.where(even, 1, 0) + 2)
+    greet(near, down, jnp.logical_and(even, blk >= 4))
+    for k in range(1, n_blk):
+        greet(ready, lax.rem(blk + n_blk - k, n_blk), jnp.logical_and(blk >= k, even) if k == 1 else blk >= k)
+
+    def send(cond, copies, held=None):
+        @pl.when(cond)
+        def _():
+            if held is not None:
+                pl.semaphore_wait(held, 1)
+            for copy in copies:
+                copy.start()
+
+    front = blk < 2
+    rear = jnp.logical_not(front)
+    send(even, [slots[0], ups[0]])
+    send(odd, [slots[1], dns[0]])
+
     for load in loads[3:]:
         load.wait()
-    for d in range(3):
-        gather(5 + d, mean[d])
-    gather(8, sound[...])
-
     cells = 2 * per_span
-    col = lax.broadcasted_iota(jnp.int32, (elems, 128), 1)
-    cell = lax.rem(col, cells)
-    first_lane = lax.rem(cell, per_span) * axial + half
-    elem = lax.broadcasted_iota(jnp.int32, (elems, 128), 0)
-    own_side = jnp.where(elem == first_lane - 1 + cell // per_span, 1.0, 0.0).astype(BF16)
-    far_side = jnp.where(elem == first_lane - cell // per_span, 1.0, 0.0).astype(BF16)
     lane = lax.broadcasted_iota(jnp.int32, (1, 128), 1)
     lane_f, lane_cell = lane // cells, lax.rem(lane, cells)
     lane_s = lax.rem(lane_cell, per_span)
@@ -195,34 +204,61 @@
     for s in range(per_span):
         code = jnp.where(lane_s == s, turns[0, s], code)
         turn_by = jnp.where(lane_s == s, offs[s], turn_by)
-    block = slice(OFF, OFF + ROWS)
-    z = jnp.zeros((ROWS, 128), F32)
+    place = jnp.zeros((1, 128), jnp.int32)
+    for c in range(cells):
+        at = (c % per_span) * axial + half - 1 + c // per_span
+        place = jnp.where(lane_cell == c, slot[:, at : at + 1], place)
+    elem = lax.broadcasted_iota(jnp.int32, (elems, 128), 0)
+    own_side = jnp.where(elem == place, 1.0, 0.0).astype(BF16)
+    state = [fields.at[k] for k in range(5)] + [mean.at[d] for d in range(3)] + [sound]
+    z = jnp.zeros((NODES, 128), F32)
     for n, f in enumerate(SENT[2]):
-        hi, lo = split(e[f, block])
+        hi, lo = split(state[f][...])
         z = jnp.where(lane_f == n, dot(hi, own_side) + dot(lo, own_side), z)
-    hi, lo = split(z)
+    hi, lo = split(jnp.concatenate([z, jnp.zeros((ROWS - NODES, 128), F32)], axis=0))
     picked = dot(pick[...], hi) + dot(pick[...], lo)
+    own_face[...] = jnp.where(stator, picked[:FROWS], picked[FROWS : 2 * FROWS])
     packet = picked[:FROWS]
     for o in range(8):
         part = picked[(o + 1) * FROWS : (o + 2) * FROWS]
         packet = jnp.where(jnp.logical_and(jnp.logical_not(stator), code == o), part, packet)
     half_rows = FROWS // 2
     pk[...] = jnp.where(lane < 64, packet[:half_rows], pltpu.roll(packet[half_rows:], 64, 1))
+    if_copies = [
+        remote(pk, gath.at[k - 1], if_ss.at[k - 1], if_rs.at[k - 1], {"blk": lax.rem(blk + k, n_blk)})
+        for k in range(1, n_blk)
+    ]
+    for k, copy in enumerate(if_copies, 1):
+        send(blk + k >= n_blk, [copy])
+    send(jnp.logical_and(even, front), [ups[1]])
+    send(jnp.logical_and(odd, front), [dns[1]])
+    send(jnp.logical_and(even, rear), [slots[1], dns[0]])
+    send(jnp.logical_and(jnp.logical_and(odd, rear), blk < n_blk - 1), [slots[0], ups[0]], near)
+    send(blk == n_blk - 1, [slots[0], ups[0]])
+
+    rows_i = lax.broadcasted_iota(jnp.int32, (elems, elems), 0)
+    perm[...] = jnp.where(rows_i == slot[...], 1.0, 0.0).astype(BF16)
+
+    def gather(f, value):
+        hi, lo = split(value)
+        e[f, :OFF] = jnp.zeros((OFF, elems), F32)
+        e[f, OFF + 120 :] = jnp.zeros((e.shape[1] - OFF - 120, elems), F32)
+        e[f, OFF : OFF + NODES] = dot(hi, perm[...]) + dot(lo, perm[...])
+
+    for f in range(9):
+        gather(f, state[f][...])
+
+    block = slice(OFF, OFF + ROWS)
     for n, f in enumerate(SENT[1]):
         for i in range(N1):
             at = OFF + i * FACE
             sp_send[0, n, i * N1 : (i + 1) * N1] = e[f, at + 20 : at + 25, elems - axial :]
             sp_send[1, n, i * N1 : (i + 1) * N1] = e[f, at : at + 5, :axial]
-    if_copies = [
-        start(pk, gath.at[k - 1], if_ss.at[k - 1], if_rs.at[k - 1], {"blk": lax.rem(blk + k, n_blk)})
-        for k in range(1, n_blk)
-    ]
-    sp_up = start(sp_send.at[0], sp_recv.at[0], sp_ss.at[0], sp_rs.at[0], {"span": right})
-    sp_dn = start(sp_send.at[1], sp_recv.at[1], sp_ss.at[1], sp_rs.at[1], {"span": left})
-    th_rest = start(
-        th_send.at[1, EARLY:], th_recv.at[1, EARLY:], th_ss.at[4], th_rs.at[4], {"blk": down}
-    )
-
+    sp_up = remote(sp_send.at[0], sp_recv.at[0], sp_ss.at[0], sp_rs.at[0], {"span": right})
+    sp_dn = remote(sp_send.at[1], sp_recv.at[1], sp_ss.at[1], sp_rs.at[1], {"span": left})
+    inner_hi, inner_lo = slab < n_span - 1, slab > 0
+    send(inner_hi, [sp_up])
+    send(inner_lo, [sp_dn])
     for s in range(per_span):
         ln = slice(s * axial, (s + 1) * axial)
         for d in range(3):
@@ -235,7 +271,20 @@
         at = slice(k * elems, (k + 1) * elems)
         rates[k] = dot(w_hi[...], fb[:, at]) + dot(w_lo[...], fb[: 3 * ROWS, at])
 
-    for side, copy in enumerate((slot_up, slot_dn)):
+    above = n_blk - 1 - blk - jnp.where(even, 1, 0)
+
+    @pl.when(above > 0)
+    def _():
+        pl.semaphore_wait(ready, above)
+
+    for k, copy in enumerate(if_copies, 1):
+        send(blk + k < n_blk, [copy])
+    send(jnp.logical_and(even, front), [ups[2], slots[1], *dns])
+    send(jnp.logical_and(odd, front), [dns[2], slots[0], *ups])
+    send(jnp.logical_and(even, rear), [*dns[1:], *ups[1:]])
+    send(jnp.logical_and(odd, rear), [*ups[1:], *dns[1:]])
+
+    for side, copy in enumerate(slots):
         copy.wait()
         far = jnp.where(rows_i == far_slot[side], 1.0, 0.0).astype(BF16)
         cross[side] = dot_t(far, perm[...]).astype(BF16)
@@ -243,8 +292,17 @@
     row = lax.broadcasted_iota(jnp.int32, (ROWS, axial), 0)
     a_id = lax.broadcasted_iota(jnp.int32, (ROWS, axial), 1)
     k_id = lax.rem(row // N1, N1)
-    sp_up.wait()
-    sp_dn.wait()
+
+    @pl.when(inner_hi)
+    def _():
+        sp_up.wait_send()
+        sp_dn.wait_recv()
+
+    @pl.when(inner_lo)
+    def _():
+        sp_dn.wait_send()
+        sp_up.wait_recv()
+
     for n in range(7):
         for i in range(N1):
             at = i * FACE
@@ -271,22 +329,6 @@
         for k, v in enumerate(correction(own, outer, sign, 1)):
             rates[k, :, ln] += jnp.where(face, v, 0.0)
 
-    for copy in if_copies:
-        copy.wait()
-    steps = jnp.where(stator, turn_by, lax.rem(n_blk - turn_by, n_blk))
-    chosen = pk[...]
-    for k in range(1, n_blk):
-        chosen = jnp.where(steps == k, gath[k - 1], chosen)
-    hi, lo = split(jnp.concatenate([chosen, pltpu.roll(chosen, 64, 1)], axis=0))
-    placed = dot(place[...], hi) + dot(place[...], lo)
-    turned = placed[:ROWS]
-    for o in range(8):
-        part = placed[(o + 1) * ROWS : (o + 2) * ROWS]
-        turned = jnp.where(jnp.logical_and(stator, code == o), part, turned)
-    for n in range(7):
-        hi, lo = split(jnp.where(lane_f == n, turned, 0.0))
-        iface[n] = dot_t(hi, far_side) + dot_t(lo, far_side)
-
     l_id = lax.rem(row, N1)
     low = l_id == 0
     face = jnp.logical_and(jnp.logical_or(low, l_id == N1 - 1), row < NODES)
@@ -300,7 +342,7 @@
         for n, f in enumerate(SENT[2]):
             lo_v = pltpu.roll(e[f, OFF + 4 : OFF + 4 + ROWS, ln], 1, 1)
             hi_v = pltpu.roll(e[f, OFF - 4 : OFF - 4 + ROWS, ln], axial - 1, 1)
-            v = jnp.where(slides, iface[n, :, ln], jnp.where(low, lo_v, hi_v))
+            v = jnp.where(slides, own[n], jnp.where(low, lo_v, hi_v))
             outer.append(jnp.where(ends, own[n] if n > 4 else 0.0, v))
         for k, v in enumerate(correction(own, outer, sign, 2)):
             rates[k, :, ln] += jnp.where(face, v, 0.0)
@@ -309,28 +351,62 @@
         hi, lo = split(rates[k])
         out[k] = (dot_t(hi, perm[...]) + dot_t(lo, perm[...]))[:NODES]
 
-    def theta(side, first, sgn):
-        hi, lo = split(th_recv[side, : 7 * FACE])
-        th_out[: 7 * FACE] = dot(hi, cross[side]) + dot(lo, cross[side])
-        own = [ref[first : first + FACE] for ref in theta_own]
-        outer = [th_out[n * FACE : (n + 1) * FACE] for n in range(7)]
-        for k, v in enumerate(correction(own, outer, sgn, 0)):
-            out[k, first : first + FACE] += v
-
-    th_up.wait()
-    theta(0, 0, -1.0)
-    th_dn.wait()
-    th_rest.wait()
-    theta(1, last, 1.0)
+    for copy in if_copies:
+        copy.wait()
+    steps = jnp.where(stator, turn_by, lax.rem(n_blk - turn_by, n_blk))
+    chosen = pk[...]
+    for k in range(1, n_blk):
+        chosen = jnp.where(steps == k, gath[k - 1], chosen)
+    chosen = jnp.concatenate([chosen, pltpu.roll(chosen, 64, 1)], axis=0)
+    hi, lo = split(chosen)
+    parts = dot(turn[...], hi) + dot(turn[...], lo)
+    for o in range(8):
+        chosen = jnp.where(jnp.logical_and(stator, code == o), parts[o * FROWS : (o + 1) * FROWS], chosen)
+    outer = jnp.where(stator, pltpu.roll(chosen, 128 - per_span, 1), pltpu.roll(chosen, per_span, 1))
+
+    def traces(x):
+        return [x if n == 0 else pltpu.roll(x, 128 - n * cells, 1) for n in range(7)]
+
+    sgn = jnp.where(stator, 1.0, -1.0)
+    for k, v in enumerate(correction(traces(own_face[...]), traces(outer), sgn, 2)):
+        at = slice(k * 128, (k + 1) * 128)
+        slide[:FROWS, at] = jnp.where(lane < per_span, v, 0.0)
+        slide[FROWS:, at] = jnp.where(jnp.logical_and(lane >= per_span, lane < cells), v, 0.0)
+    hi, lo = split(slide[...])
+    jumps = dot(put[...], hi) + dot(put[...], lo)
+    for k in range(5):
+        hi, lo = split(jumps[:, k * 128 : (k + 1) * 128])
+        out[k] += (dot_t(hi, own_side) + dot_t(lo, own_side))[:NODES]
+
+    def theta(side, first, sgn, copies):
+        for (a, b), copy in zip(GROUPS, copies):
+            copy.wait()
+            rows = slice(7 * a, 7 * b)
+            hi, lo = split(th_recv[side, rows])
+            th_out[rows] = dot(hi, cross[side]) + dot(lo, cross[side])
+            own = [ref[first + a : first + b] for ref in theta_own]
+            outer = [th_out[7 * a + n * (b - a) : 7 * a + (n + 1) * (b - a)] for n in range(7)]
+            for k, v in enumerate(correction(own, outer, sgn, 0)):
+                out[k, first + a : first + b] += v
+
+    @pl.when(even)
+    def _():
+        theta(0, 0, -1.0, ups)
+        theta(1, last, 1.0, dns)
+
+    @pl.when(odd)
+    def _():
+        theta(1, last, 1.0, dns)
+        theta(0, 0, -1.0, ups)
 
 
 def on_device(fields, store, mean, sound, slot, turns, offs, n_blk, n_span):
     per_theta, per_span = turns.shape
-    assert per_theta == 1
+    assert per_theta == 1 and n_blk % 2 == 0
     elems = slot.shape[0]
     axial = elems // per_span
     w_hi, w_lo = (jnp.asarray(t) for t in derivative_tables())
-    pick, place = (jnp.asarray(t) for t in turn_tables())
+    pick, turn, put = (jnp.asarray(t) for t in turn_tables())
     vmem = pl.BlockSpec(memory_space=pltpu.VMEM)
     hbm = pl.BlockSpec(memory_space=pl.ANY)
     smem = pl.BlockSpec(memory_space=pltpu.SMEM)
@@ -338,7 +414,7 @@
     stored = pl.pallas_call(
         functools.partial(kernel, n_blk, n_span, per_span, axial),
         out_shape=jax.ShapeDtypeStruct((5, NODES, elems), F32),
-        in_specs=[hbm] * 3 + [vmem] + [smem] * 2 + [hbm] * 4,
+        in_specs=[hbm] * 3 + [vmem] + [smem] * 2 + [hbm] * 5,
         out_specs=vmem,
         scratch_shapes=[
             pltpu.VMEM((9, OFF + ROWS + 32, elems), F32),
@@ -355,16 +431,18 @@
             pltpu.VMEM((7, ROWS, axial), F32),
             pltpu.VMEM((FROWS // 2, 128), F32),
             pltpu.VMEM((n_blk - 1, FROWS // 2, 128), F32),
-            pltpu.VMEM((7, ROWS, elems), F32),
+            pltpu.VMEM((FROWS, 128), F32),
+            pltpu.VMEM((2 * FROWS, 5 * 128), F32),
             pltpu.VMEM(fields.shape, F32),
             pltpu.VMEM(mean.shape, F32),
             pltpu.VMEM(sound.shape, F32),
-            *(pltpu.VMEM(t.shape, BF16) for t in (w_hi, w_lo, pick, place)),
-            dma((5,)), dma((5,)), dma((2,)), dma((2,)), dma((n_blk - 1,)), dma((n_blk - 1,)),
-            dma((8,)),
+            *(pltpu.VMEM(t.shape, BF16) for t in (w_hi, w_lo, pick, turn, put)),
+            dma((2, len(GROUPS))), dma((2, len(GROUPS))), dma((2,)), dma((2,)), dma((2,)), dma((2,)),
+            dma((n_blk - 1,)), dma((n_blk - 1,)), dma((9,)),
+            pltpu.SemaphoreType.REGULAR, pltpu.SemaphoreType.REGULAR,
         ],
         compiler_params=pltpu.CompilerParams(collective_id=0, has_side_effects=True),
-    )(fields, mean, sound, slot.reshape(1, elems), turns, offs, w_hi, w_lo, pick, place)
+    )(fields, mean, sound, slot.reshape(1, elems), turns, offs, w_hi, w_lo, pick, turn, put)
     store_next = section_decay * store + time_step * stored
     return fields + section_gain * store_next, store_next
 

time: 33.7 us -> 29 us (0.86)
  Pallas kernels: 29.6 us -> 24.5 us
    pallas_call x1, Pallas kernels: 29.6 us -> 24.5 us  [on_device(): pl.pallas_call(functools.partial(kernel, n_blk, n_span, per_span, axial),...]
where the time goes in v1:
time: 29 us; the launch traced here: 28.6 us
  Pallas kernels  24.5 us (84%)
  other arithmetic  3.38 us (12%)
  between operations  0.67 us (2%)
    pallas_call x1, Pallas kernels, on_device(): pl.pallas_call(functools.partial(kernel, n_blk, n_span, per_span, axial),...  24.5 us
    add x1, other arithmetic, on_device(): return (fields + section_gain * store_next, store_next)  3.38 us

profile of v1, /device:TPU:0, one launch (start us, length us, event | category | flops | bytes accessed | tf_op | source)
XLA Modules:
  0.0 28.6 jit_solution(16049668668300215347)
XLA Ops:
  0.6 0.0 copy-start
  0.6 0.0 copy-start.1
  0.7 24.5 %shard_map.131 = f32[5,125,512]{2,1,0:T(8,128)} custom-call(f32[5,125,512]{2,1,0:T(8,128)} %fields_in.1, f32[3,125,512]{2,1,0:T(8,128)} %mean_in.1, f32[125,512]{1,0:T(8,128)} %sound_in.1, s32[1,512]{1,0:T(1,128)} %bitcast.1, s32[1,4]{1,0:T(1,128)} %turns.1, s32[4]{0:T(128)} %offs.1, bf16[128,768]{1,0:T(8,128)(2,1)} %constant.16.clone.w_hi_in, ...), custom_call_target="tpu_custom_call" | custom-call | tf_op jit(solution)/shard_map/pallas_call | solution.py:414
  25.2 0.0 copy-done
  25.2 0.0 copy-done.1
  25.2 3.4 %multiply_add_fusion = (f32[5,125,512]{2,1,0:T(8,128)}, f32[5,125,512]{2,1,0:T(8,128)}) fusion(f32[5,125,512]{2,1,0:T(8,128)S(1)} %copy-done, f32[5,125,512]{2,1,0:T(8,128)} %shard_map.131, f32[5,125,512]{2,1,0:T(8,128)S(1)} %copy-done.1), kind=kLoop, calls=%fused_computation | loop fusion | flops 1600000 | bytes 6400000 | tf_op jit(solution)/shard_map/add | solution.py:447
Async XLA Ops:
  0.6 24.6 %copy-start = (f32[5,125,512]{2,1,0:T(8,128)S(1)}, f32[5,125,512]{2,1,0:T(8,128)}, u32[]{:S(2)}) copy-start(f32[5,125,512]{2,1,0:T(8,128)} %fields_in.1) | copy-start | bytes 3840004
  0.6 24.6 %copy-start.1 = (f32[5,125,512]{2,1,0:T(8,128)S(1)}, f32[5,125,512]{2,1,0:T(8,128)}, u32[]{:S(2)}) copy-start(f32[5,125,512]{2,1,0:T(8,128)} %param.13) | copy-start | bytes 3840004

commit v2 on v1

--- a/solution.py
+++ b/solution.py
@@ -15,7 +15,9 @@
 ROWS = 128
 OFF = 32
 FROWS = 32
-GROUPS = ((0, 8), (8, 16), (16, 25))
+GROUPS = ((0, 9), (9, 17), (17, 25))
+FIRST = GROUPS[0][1]
+REST = FACE - FIRST
 SENT = ((0, 1, 2, 3, 4, 5, 8), (0, 1, 2, 3, 4, 6, 8), (0, 1, 2, 3, 4, 7, 8))
 
 section_decay = -567301805773.0 / 1357537059087.0
@@ -110,12 +112,16 @@
     return [w * (sign * (fo[k] - fx[k]) + reach * (outer[k] - own[k])) for k in range(5)]
 
 
+def merge(q, m, c, reach, d):
+    return [f + reach * v for f, v in zip(flux([*q, m, c], d), q)]
+
+
 def kernel(
     n_blk, n_span, per_span, axial, fields_in, mean_in, sound_in, slot, turns, offs, w_hi_in, w_lo_in,
     pick_in, turn_in, put_in,
-    out, e, perm, fb, rates, th_send, th_recv, th_out, far_slot, cross, sp_send, sp_recv, sp_rows, pk,
+    out_hbm, out, e, perm, fb, rates, th_send, th_recv, th_out, rate_send, rate_recv, up_send, up_recv, up_own, fix, far_slot, cross, sp_send, sp_recv, sp_rows, pk,
     gath, own_face, slide, fields, mean, sound, w_hi, w_lo, pick, turn, put,
-    th_ss, th_rs, sl_ss, sl_rs, sp_ss, sp_rs, if_ss, if_rs, loaded, ready, near,
+    th_ss, th_rs, ra_ss, ra_rs, up_ss, up_rs, sl_ss, sl_rs, sp_ss, sp_rs, if_ss, if_rs, loaded, saved, ready, near,
 ):
     elems = per_span * axial
     half = axial // 2
@@ -125,7 +131,7 @@
 
     first = pl.ds(0, 1)
     pairs = (
-        (fields_in, fields), (mean_in.at[first], mean.at[first]), (sound_in, sound),
+        (mean_in.at[first], mean.at[first]), (sound_in, sound), (fields_in, fields),
         (mean_in.at[pl.ds(1, 2)], mean.at[pl.ds(1, 2)]), (w_hi_in, w_hi), (w_lo_in, w_lo),
         (pick_in, pick), (turn_in, turn), (put_in, put),
     )
@@ -149,13 +155,13 @@
 
     last = NODES - FACE
     theta_own = [fields.at[k] for k in range(5)] + [mean.at[0], sound]
-    for load in loads[:3]:
-        load.wait()
-    for a, b in GROUPS:
-        for n, ref in enumerate(theta_own):
-            at = 7 * a + n * (b - a)
-            th_send[0, at : at + b - a] = ref[last + a : last + b]
-            th_send[1, at : at + b - a] = ref[a:b]
+    near_side = lax.rem(blk, 2)
+    far_side = 1 - near_side
+    near_blk = jnp.where(even, up, down)
+    far_blk = jnp.where(even, down, up)
+    tail = blk == n_blk - 1
+    wrap = jnp.logical_or(blk == 0, tail)
+    inner = jnp.logical_not(wrap)
 
     def remote(src, dst, ss, rs, target):
         return pltpu.make_async_remote_copy(
@@ -164,20 +170,19 @@
         )
 
     def flow(side, target):
-        at = [slice(7 * a, 7 * b + (b == FACE)) for a, b in GROUPS]
-        return [
-            remote(th_send.at[side, r], th_recv.at[side, r], th_ss.at[side, g], th_rs.at[side, g], {"blk": target})
-            for g, r in enumerate(at)
-        ]
-
-    ups, dns = flow(0, up), flow(1, down)
-    slots = [
-        remote(slot, far_slot.at[n], sl_ss.at[n], sl_rs.at[n], {"blk": t}) for n, t in enumerate((up, down))
-    ]
-    pl.semaphore_wait(barrier, blk + jnp.where(even, 1, 0) + 2)
-    greet(near, down, jnp.logical_and(even, blk >= 4))
-    for k in range(1, n_blk):
-        greet(ready, lax.rem(blk + n_blk - k, n_blk), jnp.logical_and(blk >= k, even) if k == 1 else blk >= k)
+        to = {"blk": target}
+        slot_copy = remote(slot, far_slot.at[side], sl_ss.at[side], sl_rs.at[side], to)
+        rate = remote(rate_send.at[side], rate_recv.at[side], ra_ss.at[side], ra_rs.at[side], to)
+        full = []
+        for g, (a, b) in enumerate(GROUPS):
+            r = slice(7 * a + (g > 0), 7 * b + 1)
+            full.append(remote(th_send.at[side, r], th_recv.at[side, r], th_ss.at[side, g], th_rs.at[side, g], to))
+        half_size = 5 * REST // 2
+        part = []
+        for g in range(2):
+            r = slice(g * half_size, (g + 1) * half_size)
+            part.append(remote(up_send.at[side, r], up_recv.at[side, r], up_ss.at[side, g], up_rs.at[side, g], to))
+        return slot_copy, rate, full, part
 
     def send(cond, copies, held=None):
         @pl.when(cond)
@@ -187,10 +192,63 @@
             for copy in copies:
                 copy.start()
 
-    front = blk < 2
-    rear = jnp.logical_not(front)
-    send(even, [slots[0], ups[0]])
-    send(odd, [slots[1], dns[0]])
+    pl.semaphore_wait(barrier, blk + jnp.where(even, 1, 0) + 2)
+    greet(near, down, jnp.logical_and(even, blk > 0))
+    for k in range(1, n_blk):
+        greet(ready, lax.rem(blk + n_blk - k, n_blk), jnp.logical_and(blk >= k, even) if k == 1 else blk >= k)
+    near_slot, near_rate, near_full, near_part = flow(near_side, near_blk)
+    far_slot_copy, far_rate, far_full, far_part = flow(far_side, far_blk)
+    for load in loads[:2]:
+        load.wait()
+    for side, at in enumerate((last, 0)):
+        rows = slice(at + FIRST, at + FACE)
+        rate_send[side] = jnp.abs(mean[0, rows]) + sound[rows]
+    near_slot.start()
+    near_rate.start()
+    send(jnp.logical_and(even, inner), [far_slot_copy, far_rate])
+    loads[2].wait()
+    for g, (a, b) in enumerate(GROUPS):
+        for n, ref in enumerate(theta_own):
+            at = 7 * a + (g > 0) + n * (b - a)
+            th_send[0, at : at + b - a] = ref[last + a : last + b]
+            th_send[1, at : at + b - a] = ref[a:b]
+    send(tail, [far_slot_copy, *far_full])
+    near_full[0].start()
+    send(jnp.logical_and(even, inner), [far_full[0]])
+
+    rows_i = lax.broadcasted_iota(jnp.int32, (elems, elems), 0)
+    perm[...] = jnp.where(rows_i == slot[...], 1.0, 0.0).astype(BF16)
+
+
+    def link(side):
+        hi, lo = split(jnp.broadcast_to(far_slot[side].astype(F32), (8, elems)))
+        source = (dot_t(hi, perm[...]) + dot_t(lo, perm[...]))[:1].astype(jnp.int32)
+        cross[side] = jnp.where(rows_i == source, 1.0, 0.0).astype(BF16)
+
+    def blend(side):
+        sgn = jnp.where(side == 0, 1.0, -1.0)
+        hi, lo = split(rate_recv[1 - side])
+        there = dot(hi, cross[1 - side]) + dot(lo, cross[1 - side])
+        reach = sgn * jnp.maximum(rate_send[side], there)
+        for g, (a, b) in enumerate(GROUPS[1:]):
+            at = 7 * a + 1
+            own = [th_send[side, at + n * (b - a) : at + (n + 1) * (b - a)] for n in range(7)]
+            speed = reach[a - FIRST : b - FIRST]
+            for sign, ref in ((1.0, up_send), (-1.0, up_own)):
+                for k, v in enumerate(merge(own[:5], own[5], own[6], sign * speed, 0)):
+                    to = 5 * (a - FIRST) + k * (b - a)
+                    ref[side, to : to + b - a] = v
+
+    in_near = flow(far_side, near_blk)
+    in_far = flow(near_side, far_blk)
+    def settle_near():
+        in_near[0].wait_recv()
+        link(far_side)
+        in_near[1].wait_recv()
+        blend(near_side)
+        near_part[0].start()
+        near_part[1].start()
+
 
     for load in loads[3:]:
         load.wait()
@@ -230,14 +288,7 @@
     ]
     for k, copy in enumerate(if_copies, 1):
         send(blk + k >= n_blk, [copy])
-    send(jnp.logical_and(even, front), [ups[1]])
-    send(jnp.logical_and(odd, front), [dns[1]])
-    send(jnp.logical_and(even, rear), [slots[1], dns[0]])
-    send(jnp.logical_and(jnp.logical_and(odd, rear), blk < n_blk - 1), [slots[0], ups[0]], near)
-    send(blk == n_blk - 1, [slots[0], ups[0]])
-
-    rows_i = lax.broadcasted_iota(jnp.int32, (elems, elems), 0)
-    perm[...] = jnp.where(rows_i == slot[...], 1.0, 0.0).astype(BF16)
+    send(jnp.logical_and(odd, inner), [far_slot_copy, far_rate, far_full[0]], near)
 
     def gather(f, value):
         hi, lo = split(value)
@@ -259,6 +310,26 @@
     inner_hi, inner_lo = slab < n_span - 1, slab > 0
     send(inner_hi, [sp_up])
     send(inner_lo, [sp_dn])
+
+    above = n_blk - 1 - blk - jnp.where(even, 1, 0)
+
+    @pl.when(above > 0)
+    def _():
+        pl.semaphore_wait(ready, above)
+
+    for k, copy in enumerate(if_copies, 1):
+        send(blk + k < n_blk, [copy])
+    send(blk == 0, [far_slot_copy, *far_full])
+    settle_near()
+    @pl.when(inner)
+    def _():
+        in_far[0].wait_recv()
+        link(near_side)
+        in_far[1].wait_recv()
+        blend(far_side)
+        far_part[0].start()
+        far_part[1].start()
+
     for s in range(per_span):
         ln = slice(s * axial, (s + 1) * axial)
         for d in range(3):
@@ -271,23 +342,6 @@
         at = slice(k * elems, (k + 1) * elems)
         rates[k] = dot(w_hi[...], fb[:, at]) + dot(w_lo[...], fb[: 3 * ROWS, at])
 
-    above = n_blk - 1 - blk - jnp.where(even, 1, 0)
-
-    @pl.when(above > 0)
-    def _():
-        pl.semaphore_wait(ready, above)
-
-    for k, copy in enumerate(if_copies, 1):
-        send(blk + k < n_blk, [copy])
-    send(jnp.logical_and(even, front), [ups[2], slots[1], *dns])
-    send(jnp.logical_and(odd, front), [dns[2], slots[0], *ups])
-    send(jnp.logical_and(even, rear), [*dns[1:], *ups[1:]])
-    send(jnp.logical_and(odd, rear), [*ups[1:], *dns[1:]])
-
-    for side, copy in enumerate(slots):
-        copy.wait()
-        far = jnp.where(rows_i == far_slot[side], 1.0, 0.0).astype(BF16)
-        cross[side] = dot_t(far, perm[...]).astype(BF16)
 
     row = lax.broadcasted_iota(jnp.int32, (ROWS, axial), 0)
     a_id = lax.broadcasted_iota(jnp.int32, (ROWS, axial), 1)
@@ -351,6 +405,11 @@
         hi, lo = split(rates[k])
         out[k] = (dot_t(hi, perm[...]) + dot_t(lo, perm[...]))[:NODES]
 
+    @pl.when(wrap)
+    def _():
+        in_far[0].wait_recv()
+        link(near_side)
+
     for copy in if_copies:
         copy.wait()
     steps = jnp.where(stator, turn_by, lax.rem(n_blk - turn_by, n_blk))
@@ -378,26 +437,88 @@
         hi, lo = split(jumps[:, k * 128 : (k + 1) * 128])
         out[k] += (dot_t(hi, own_side) + dot_t(lo, own_side))[:NODES]
 
-    def theta(side, first, sgn, copies):
-        for (a, b), copy in zip(GROUPS, copies):
-            copy.wait()
-            rows = slice(7 * a, 7 * b)
-            hi, lo = split(th_recv[side, rows])
-            th_out[rows] = dot(hi, cross[side]) + dot(lo, cross[side])
-            own = [ref[first + a : first + b] for ref in theta_own]
-            outer = [th_out[7 * a + n * (b - a) : 7 * a + (n + 1) * (b - a)] for n in range(7)]
-            for k, v in enumerate(correction(own, outer, sgn, 0)):
-                out[k, first + a : first + b] += v
-
-    @pl.when(even)
-    def _():
-        theta(0, 0, -1.0, ups)
-        theta(1, last, 1.0, dns)
-
-    @pl.when(odd)
-    def _():
-        theta(1, last, 1.0, dns)
-        theta(0, 0, -1.0, ups)
+    mid = pltpu.make_async_copy(out.at[:, 32:96], out_hbm.at[:5, 32:96], saved.at[0])
+    mid.start()
+
+    def add(side, a, b):
+        for at, cond in ((0, side == 0), (last, side == 1)):
+            @pl.when(cond)
+            def _():
+                for k in range(5):
+                    out[k, at + a : at + b] += fix[k, : b - a]
+
+    def theta(side, g, copy):
+        copy.wait_recv()
+        a, b = GROUPS[g]
+        at = 7 * a + (g > 0)
+        hi, lo = split(th_recv[side, at : at + 7 * (b - a)])
+        th_out[: 7 * (b - a)] = dot(hi, cross[side]) + dot(lo, cross[side])
+        own = [th_send[1 - side, at + n * (b - a) : at + (n + 1) * (b - a)] for n in range(7)]
+        outer = [th_out[n * (b - a) : (n + 1) * (b - a)] for n in range(7)]
+        sgn = jnp.where(side == 0, -1.0, 1.0)
+        for k, v in enumerate(correction(own, outer, sgn, 0)):
+            fix[k, : b - a] = v
+        add(side, a, b)
+
+    def blended(side, g, copy):
+        copy.wait_recv()
+        a, b = GROUPS[g]
+        at = 5 * (a - FIRST)
+        hi, lo = split(up_recv[side, at : at + 5 * (b - a)])
+        there = dot(hi, cross[side]) + dot(lo, cross[side])
+        w = 0.5 * metric_scale[0] / end_weight * jnp.where(side == 0, -1.0, 1.0)
+        for k in range(5):
+            n = slice(k * (b - a), (k + 1) * (b - a))
+            fix[k, : b - a] = w * (up_own[1 - side, at + k * (b - a) : at + (k + 1) * (b - a)] - there[n])
+        add(side, a, b)
+
+    theta(far_side, 0, in_near[2][0])
+    theta(near_side, 0, in_far[2][0])
+
+    @pl.when(wrap)
+    def _():
+        for g in (1, 2):
+            blended(far_side, g, in_near[3][g - 1])
+        for g in (1, 2):
+            theta(near_side, g, in_far[2][g])
+            far_full[g].wait_send()
+
+    @pl.when(inner)
+    def _():
+        blended(far_side, 1, in_near[3][0])
+        for g in (1, 2):
+            blended(near_side, g, in_far[3][g - 1])
+            far_part[g - 1].wait_send()
+        blended(far_side, 2, in_near[3][1])
+        far_rate.wait_send()
+
+    lows = pltpu.make_async_copy(out.at[:, :32], out_hbm.at[:5, :32], saved.at[1])
+    highs = pltpu.make_async_copy(out.at[:, 96:], out_hbm.at[:5, 96:], saved.at[2])
+    lows.start()
+    highs.start()
+    for copy in (near_slot, near_rate, near_full[0], *near_part, far_slot_copy, far_full[0]):
+        copy.wait_send()
+    for copy in (mid, lows, highs):
+        copy.wait()
+
+
+def finish(stored_in, fields, store, fields_out, store_out, stored, fields_next, store_next, in_sem, f_sem, s_sem):
+    count = stored.shape[0]
+    loads = [pltpu.make_async_copy(stored_in.at[k], stored.at[k], in_sem.at[k]) for k in range(count)]
+    for load in loads:
+        load.start()
+    saves = []
+    for k, load in enumerate(loads):
+        load.wait()
+        value = section_decay * store[k] + time_step * stored[k]
+        store_next[k] = value
+        fields_next[k] = fields[k] + section_gain * value
+        saves.append(pltpu.make_async_copy(store_next.at[k], store_out.at[k], s_sem.at[k]))
+        saves.append(pltpu.make_async_copy(fields_next.at[k], fields_out.at[k], f_sem.at[k]))
+        saves[-2].start()
+        saves[-1].start()
+    for save in saves:
+        save.wait()
 
 
 def on_device(fields, store, mean, sound, slot, turns, offs, n_blk, n_span):
@@ -413,10 +534,11 @@
     dma = pltpu.SemaphoreType.DMA
     stored = pl.pallas_call(
         functools.partial(kernel, n_blk, n_span, per_span, axial),
-        out_shape=jax.ShapeDtypeStruct((5, NODES, elems), F32),
+        out_shape=jax.ShapeDtypeStruct((48, NODES, elems), F32),
         in_specs=[hbm] * 3 + [vmem] + [smem] * 2 + [hbm] * 5,
-        out_specs=vmem,
+        out_specs=hbm,
         scratch_shapes=[
+            pltpu.VMEM(fields.shape, F32),
             pltpu.VMEM((9, OFF + ROWS + 32, elems), F32),
             pltpu.VMEM((elems, elems), BF16),
             pltpu.VMEM((6 * ROWS, 5 * elems), BF16),
@@ -424,6 +546,12 @@
             pltpu.VMEM((2, 7 * FACE + 1, elems), F32),
             pltpu.VMEM((2, 7 * FACE + 1, elems), F32),
             pltpu.VMEM((7 * FACE + 1, elems), F32),
+            pltpu.VMEM((2, REST, elems), F32),
+            pltpu.VMEM((2, REST, elems), F32),
+            pltpu.VMEM((2, 5 * REST, elems), F32),
+            pltpu.VMEM((2, 5 * REST, elems), F32),
+            pltpu.VMEM((2, 5 * REST, elems), F32),
+            pltpu.VMEM((5, FROWS // 2, elems), F32),
             pltpu.VMEM((2, 1, elems), jnp.int32),
             pltpu.VMEM((2, elems, elems), BF16),
             pltpu.VMEM((2, 7, FROWS, axial), F32),
@@ -437,14 +565,23 @@
             pltpu.VMEM(mean.shape, F32),
             pltpu.VMEM(sound.shape, F32),
             *(pltpu.VMEM(t.shape, BF16) for t in (w_hi, w_lo, pick, turn, put)),
-            dma((2, len(GROUPS))), dma((2, len(GROUPS))), dma((2,)), dma((2,)), dma((2,)), dma((2,)),
-            dma((n_blk - 1,)), dma((n_blk - 1,)), dma((9,)),
+            dma((2, len(GROUPS))), dma((2, len(GROUPS))), dma((2,)), dma((2,)), dma((2, 2)), dma((2, 2)),
+            dma((2,)), dma((2,)), dma((2,)), dma((2,)),
+            dma((n_blk - 1,)), dma((n_blk - 1,)), dma((9,)), dma((3,)),
             pltpu.SemaphoreType.REGULAR, pltpu.SemaphoreType.REGULAR,
         ],
         compiler_params=pltpu.CompilerParams(collective_id=0, has_side_effects=True),
     )(fields, mean, sound, slot.reshape(1, elems), turns, offs, w_hi, w_lo, pick, turn, put)
-    store_next = section_decay * store + time_step * stored
-    return fields + section_gain * store_next, store_next
+    shape = jax.ShapeDtypeStruct(fields.shape, F32)
+    count = fields.shape[0]
+    return pl.pallas_call(
+        finish,
+        out_shape=(shape, shape),
+        in_specs=[hbm, vmem, vmem],
+        out_specs=(hbm, hbm),
+        scratch_shapes=[pltpu.VMEM(fields.shape, F32)] * 3 + [dma((count,))] * 3,
+        compiler_params=pltpu.CompilerParams(vmem_limit_bytes=50 * 2**20),
+    )(stored, fields, store)
 
 
 def solution(mesh):

time: 29 us -> 27.8 us (0.959); the launches traced: 28.6 us -> 27.7 us
  other arithmetic: 3.38 us -> 0 us
  Pallas kernels: 24.5 us -> 27 us
    add x1 -> x0, other arithmetic: 3.38 us -> none  [on_device(): return (fields + section_gain * store_next, store_next)]
    pallas_call x0 -> x1, Pallas kernels: none -> 2.63 us  [on_device(): pl.pallas_call(finish, out_shape=(shape, shape), in_specs=[hbm, vmem, vme...]
where the time goes in v2:
time: 27.8 us; the launch traced here: 27.7 us
  Pallas kernels  27 us (97%)
  between operations  0.67 us (2%)
    pallas_call x1, Pallas kernels, on_device(): pl.pallas_call(functools.partial(kernel, n_blk, n_span, per_span, axial),...  24.4 us
    pallas_call x1, Pallas kernels, on_device(): pl.pallas_call(finish, out_shape=(shape, shape), in_specs=[hbm, vmem, vme...  2.63 us

profile of v2, /device:TPU:0, one launch (start us, length us, event | category | flops | bytes accessed | tf_op | source)
XLA Modules:
  0.0 27.7 jit_solution(9752501709242753038)
XLA Ops:
  0.6 0.0 copy-start
  0.6 0.0 copy-start.1
  0.7 24.4 %shard_map.131.stored_in = f32[48,125,512]{2,1,0:T(8,128)} custom-call(f32[5,125,512]{2,1,0:T(8,128)} %fields.1, f32[3,125,512]{2,1,0:T(8,128)} %mean_in.1, f32[125,512]{1,0:T(8,128)} %sound_in.1, s32[1,512]{1,0:T(1,128)} %bitcast.1, s32[1,4]{1,0:T(1,128)} %turns.1, s32[4]{0:T(128)} %offs.1, bf16[128,768]{1,0:T(8,128)(2,1)} %constant.10.clone.w_hi_in, ...), custom_call_target="tpu_custom_call" | custom-call | tf_op jit(solution)/shard_map/pallas_call | solution.py:535
  25.0 0.0 copy-done
  25.1 0.0 copy-done.1
  25.1 2.6 %shard_map.132 = (f32[5,125,512]{2,1,0:T(8,128)}, f32[5,125,512]{2,1,0:T(8,128)}) custom-call(f32[48,125,512]{2,1,0:T(8,128)} %shard_map.131.stored_in, f32[5,125,512]{2,1,0:T(8,128)S(1)} %copy-done, f32[5,125,512]{2,1,0:T(8,128)S(1)} %copy-done.1), custom_call_target="tpu_custom_call" | custom-call | tf_op jit(solution)/shard_map/pallas_call | solution.py:577
Async XLA Ops:
  0.6 24.4 %copy-start = (f32[5,125,512]{2,1,0:T(8,128)S(1)}, f32[5,125,512]{2,1,0:T(8,128)}, u32[]{:S(2)}) copy-start(f32[5,125,512]{2,1,0:T(8,128)} %fields.1) | copy-start | bytes 3840004
  0.6 24.4 %copy-start.1 = (f32[5,125,512]{2,1,0:T(8,128)S(1)}, f32[5,125,512]{2,1,0:T(8,128)}, u32[]{:S(2)}) copy-start(f32[5,125,512]{2,1,0:T(8,128)} %store.1) | copy-start | bytes 3840004

commit v3 on v2

--- a/solution.py
+++ b/solution.py
@@ -205,14 +205,15 @@
         rate_send[side] = jnp.abs(mean[0, rows]) + sound[rows]
     near_slot.start()
     near_rate.start()
-    send(jnp.logical_and(even, inner), [far_slot_copy, far_rate])
+    low_far = jnp.logical_or(jnp.logical_and(even, inner), tail)
+    send(low_far, [far_slot_copy, far_rate])
     loads[2].wait()
     for g, (a, b) in enumerate(GROUPS):
         for n, ref in enumerate(theta_own):
             at = 7 * a + (g > 0) + n * (b - a)
             th_send[0, at : at + b - a] = ref[last + a : last + b]
             th_send[1, at : at + b - a] = ref[a:b]
-    send(tail, [far_slot_copy, *far_full])
+    send(tail, [far_full[0]])
     near_full[0].start()
     send(jnp.logical_and(even, inner), [far_full[0]])
 
@@ -317,18 +318,19 @@
     def _():
         pl.semaphore_wait(ready, above)
 
+    send(blk == 0, [far_slot_copy, far_rate, far_full[0]])
     for k, copy in enumerate(if_copies, 1):
         send(blk + k < n_blk, [copy])
-    send(blk == 0, [far_slot_copy, *far_full])
     settle_near()
-    @pl.when(inner)
-    def _():
+    def settle_far():
         in_far[0].wait_recv()
         link(near_side)
         in_far[1].wait_recv()
         blend(far_side)
         far_part[0].start()
         far_part[1].start()
+
+    pl.when(inner)(settle_far)
 
     for s in range(per_span):
         ln = slice(s * axial, (s + 1) * axial)
@@ -343,6 +345,7 @@
         rates[k] = dot(w_hi[...], fb[:, at]) + dot(w_lo[...], fb[: 3 * ROWS, at])
 
 
+    pl.when(wrap)(settle_far)
     row = lax.broadcasted_iota(jnp.int32, (ROWS, axial), 0)
     a_id = lax.broadcasted_iota(jnp.int32, (ROWS, axial), 1)
     k_id = lax.rem(row // N1, N1)
@@ -405,11 +408,6 @@
         hi, lo = split(rates[k])
         out[k] = (dot_t(hi, perm[...]) + dot_t(lo, perm[...]))[:NODES]
 
-    @pl.when(wrap)
-    def _():
-        in_far[0].wait_recv()
-        link(near_side)
-
     for copy in if_copies:
         copy.wait()
     steps = jnp.where(stator, turn_by, lax.rem(n_blk - turn_by, n_blk))
@@ -475,28 +473,16 @@
     theta(far_side, 0, in_near[2][0])
     theta(near_side, 0, in_far[2][0])
 
-    @pl.when(wrap)
-    def _():
-        for g in (1, 2):
-            blended(far_side, g, in_near[3][g - 1])
-        for g in (1, 2):
-            theta(near_side, g, in_far[2][g])
-            far_full[g].wait_send()
-
-    @pl.when(inner)
-    def _():
-        blended(far_side, 1, in_near[3][0])
-        for g in (1, 2):
-            blended(near_side, g, in_far[3][g - 1])
-            far_part[g - 1].wait_send()
-        blended(far_side, 2, in_near[3][1])
-        far_rate.wait_send()
+    blended(far_side, 1, in_near[3][0])
+    for g in (1, 2):
+        blended(near_side, g, in_far[3][g - 1])
+    blended(far_side, 2, in_near[3][1])
 
     lows = pltpu.make_async_copy(out.at[:, :32], out_hbm.at[:5, :32], saved.at[1])
     highs = pltpu.make_async_copy(out.at[:, 96:], out_hbm.at[:5, 96:], saved.at[2])
     lows.start()
     highs.start()
-    for copy in (near_slot, near_rate, near_full[0], *near_part, far_slot_copy, far_full[0]):
+    for copy in (near_slot, near_rate, near_full[0], *near_part, far_slot_copy, far_rate, far_full[0], *far_part):
         copy.wait_send()
     for copy in (mid, lows, highs):
         copy.wait()

time: 27.8 us -> 26.5 us (0.953)
  Pallas kernels: 27 us -> 25.6 us
    pallas_call x1, Pallas kernels: 24.4 us -> 23 us  [on_device(): pl.pallas_call(functools.partial(kernel, n_blk, n_span, per_span, axial),...]
where the time goes in v3:
time: 26.5 us; the launch traced here: 26.3 us
  Pallas kernels  25.6 us (97%)
  between operations  0.67 us (3%)
    pallas_call x1, Pallas kernels, on_device(): pl.pallas_call(functools.partial(kernel, n_blk, n_span, per_span, axial),...  23 us
    pallas_call x1, Pallas kernels, on_device(): pl.pallas_call(finish, out_shape=(shape, shape), in_specs=[hbm, vmem, vme...  2.63 us

profile of v3, /device:TPU:0, one launch (start us, length us, event | category | flops | bytes accessed | tf_op | source)
XLA Modules:
  0.0 26.3 jit_solution(9441543945385904046)
XLA Ops:
  0.6 0.0 copy-start
  0.6 0.0 copy-start.1
  0.7 23.0 %shard_map.131.stored_in = f32[48,125,512]{2,1,0:T(8,128)} custom-call(f32[5,125,512]{2,1,0:T(8,128)} %fields.1, f32[3,125,512]{2,1,0:T(8,128)} %mean_in.1, f32[125,512]{1,0:T(8,128)} %sound_in.1, s32[1,512]{1,0:T(1,128)} %bitcast.1, s32[1,4]{1,0:T(1,128)} %turns.1, s32[4]{0:T(128)} %offs.1, bf16[128,768]{1,0:T(8,128)(2,1)} %constant.10.clone.w_hi_in, ...), custom_call_target="tpu_custom_call" | custom-call | tf_op jit(solution)/shard_map/pallas_call | solution.py:521
  23.7 0.0 copy-done
  23.7 0.0 copy-done.1
  23.7 2.6 %shard_map.132 = (f32[5,125,512]{2,1,0:T(8,128)}, f32[5,125,512]{2,1,0:T(8,128)}) custom-call(f32[48,125,512]{2,1,0:T(8,128)} %shard_map.131.stored_in, f32[5,125,512]{2,1,0:T(8,128)S(1)} %copy-done, f32[5,125,512]{2,1,0:T(8,128)S(1)} %copy-done.1), custom_call_target="tpu_custom_call" | custom-call | tf_op jit(solution)/shard_map/pallas_call | solution.py:563
Async XLA Ops:
  0.6 23.0 %copy-start = (f32[5,125,512]{2,1,0:T(8,128)S(1)}, f32[5,125,512]{2,1,0:T(8,128)}, u32[]{:S(2)}) copy-start(f32[5,125,512]{2,1,0:T(8,128)} %fields.1) | copy-start | bytes 3840004
  0.6 23.0 %copy-start.1 = (f32[5,125,512]{2,1,0:T(8,128)S(1)}, f32[5,125,512]{2,1,0:T(8,128)}, u32[]{:S(2)}) copy-start(f32[5,125,512]{2,1,0:T(8,128)} %store.1) | copy-start | bytes 3840004

commit v4 on v3

--- a/solution.py
+++ b/solution.py
@@ -93,6 +93,13 @@
 
 def dot_t(a, b):
     return lax.dot_general(a, b, (((1,), (1,)), ((), ())), preferred_element_type=F32)
+
+
+def shuffle(x, table):
+    rows = x.shape[0]
+    hi = x.astype(BF16).astype(F32)
+    both = dot(jnp.concatenate([hi, x - hi], axis=0).astype(BF16), table)
+    return both[:rows] + both[rows:]
 
 
 def flux(state, d):
@@ -228,8 +235,7 @@
 
     def blend(side):
         sgn = jnp.where(side == 0, 1.0, -1.0)
-        hi, lo = split(rate_recv[1 - side])
-        there = dot(hi, cross[1 - side]) + dot(lo, cross[1 - side])
+        there = shuffle(rate_recv[1 - side], cross[1 - side])
         reach = sgn * jnp.maximum(rate_send[side], there)
         for g, (a, b) in enumerate(GROUPS[1:]):
             at = 7 * a + 1
@@ -312,6 +318,7 @@
     send(inner_hi, [sp_up])
     send(inner_lo, [sp_dn])
 
+    pl.when(odd)(settle_near)
     above = n_blk - 1 - blk - jnp.where(even, 1, 0)
 
     @pl.when(above > 0)
@@ -321,7 +328,7 @@
     send(blk == 0, [far_slot_copy, far_rate, far_full[0]])
     for k, copy in enumerate(if_copies, 1):
         send(blk + k < n_blk, [copy])
-    settle_near()
+    pl.when(even)(settle_near)
     def settle_far():
         in_far[0].wait_recv()
         link(near_side)
@@ -408,6 +415,40 @@
         hi, lo = split(rates[k])
         out[k] = (dot_t(hi, perm[...]) + dot_t(lo, perm[...]))[:NODES]
 
+    def add(side, a, b):
+        for at, cond in ((0, side == 0), (last, side == 1)):
+            @pl.when(cond)
+            def _():
+                for k in range(5):
+                    out[k, at + a : at + b] += fix[k, : b - a]
+
+    def theta(side, g, copy):
+        copy.wait_recv()
+        a, b = GROUPS[g]
+        at = 7 * a + (g > 0)
+        size = 7 * (b - a) + (g == 0)
+        th_out[:size] = shuffle(th_recv[side, at : at + size], cross[side])
+        own = [th_send[1 - side, at + n * (b - a) : at + (n + 1) * (b - a)] for n in range(7)]
+        outer = [th_out[n * (b - a) : (n + 1) * (b - a)] for n in range(7)]
+        sgn = jnp.where(side == 0, -1.0, 1.0)
+        for k, v in enumerate(correction(own, outer, sgn, 0)):
+            fix[k, : b - a] = v
+        add(side, a, b)
+
+    def blended(side, g, copy):
+        copy.wait_recv()
+        a, b = GROUPS[g]
+        at = 5 * (a - FIRST)
+        there = shuffle(up_recv[side, at : at + 5 * (b - a)], cross[side])
+        w = 0.5 * metric_scale[0] / end_weight * jnp.where(side == 0, -1.0, 1.0)
+        for k in range(5):
+            n = slice(k * (b - a), (k + 1) * (b - a))
+            fix[k, : b - a] = w * (up_own[1 - side, at + k * (b - a) : at + (k + 1) * (b - a)] - there[n])
+        add(side, a, b)
+
+    theta(far_side, 0, in_near[2][0])
+    theta(near_side, 0, in_far[2][0])
+
     for copy in if_copies:
         copy.wait()
     steps = jnp.where(stator, turn_by, lax.rem(n_blk - turn_by, n_blk))
@@ -437,41 +478,6 @@
 
     mid = pltpu.make_async_copy(out.at[:, 32:96], out_hbm.at[:5, 32:96], saved.at[0])
     mid.start()
-
-    def add(side, a, b):
-        for at, cond in ((0, side == 0), (last, side == 1)):
-            @pl.when(cond)
-            def _():
-                for k in range(5):
-                    out[k, at + a : at + b] += fix[k, : b - a]
-
-    def theta(side, g, copy):
-        copy.wait_recv()
-        a, b = GROUPS[g]
-        at = 7 * a + (g > 0)
-        hi, lo = split(th_recv[side, at : at + 7 * (b - a)])
-        th_out[: 7 * (b - a)] = dot(hi, cross[side]) + dot(lo, cross[side])
-        own = [th_send[1 - side, at + n * (b - a) : at + (n + 1) * (b - a)] for n in range(7)]
-        outer = [th_out[n * (b - a) : (n + 1) * (b - a)] for n in range(7)]
-        sgn = jnp.where(side == 0, -1.0, 1.0)
-        for k, v in enumerate(correction(own, outer, sgn, 0)):
-            fix[k, : b - a] = v
-        add(side, a, b)
-
-    def blended(side, g, copy):
-        copy.wait_recv()
-        a, b = GROUPS[g]
-        at = 5 * (a - FIRST)
-        hi, lo = split(up_recv[side, at : at + 5 * (b - a)])
-        there = dot(hi, cross[side]) + dot(lo, cross[side])
-        w = 0.5 * metric_scale[0] / end_weight * jnp.where(side == 0, -1.0, 1.0)
-        for k in range(5):
-            n = slice(k * (b - a), (k + 1) * (b - a))
-            fix[k, : b - a] = w * (up_own[1 - side, at + k * (b - a) : at + (k + 1) * (b - a)] - there[n])
-        add(side, a, b)
-
-    theta(far_side, 0, in_near[2][0])
-    theta(near_side, 0, in_far[2][0])
 
     blended(far_side, 1, in_near[3][0])
     for g in (1, 2):

time: 26.5 us -> 26.4 us (level)
  no operation moved by 1% of the time
where the time goes in v4:
time: 26.4 us; the launch traced here: 26.2 us
  Pallas kernels  25.6 us (97%)
  between operations  0.67 us (3%)
    pallas_call x1, Pallas kernels, on_device(): pl.pallas_call(functools.partial(kernel, n_blk, n_span, per_span, axial),...  22.9 us
    pallas_call x1, Pallas kernels, on_device(): pl.pallas_call(finish, out_shape=(shape, shape), in_specs=[hbm, vmem, vme...  2.63 us

profile of v4, /device:TPU:0, one launch (start us, length us, event | category | flops | bytes accessed | tf_op | source)
XLA Modules:
  0.0 26.2 jit_solution(565567151933650114)
XLA Ops:
  0.6 0.0 copy-start
  0.6 0.0 copy-start.1
  0.7 22.9 %shard_map.131.stored_in = f32[48,125,512]{2,1,0:T(8,128)} custom-call(f32[5,125,512]{2,1,0:T(8,128)} %fields.1, f32[3,125,512]{2,1,0:T(8,128)} %mean_in.1, f32[125,512]{1,0:T(8,128)} %sound_in.1, s32[1,512]{1,0:T(1,128)} %bitcast.1, s32[1,4]{1,0:T(1,128)} %turns.1, s32[4]{0:T(128)} %offs.1, bf16[128,768]{1,0:T(8,128)(2,1)} %constant.10.clone.w_hi_in, ...), custom_call_target="tpu_custom_call" | custom-call | tf_op jit(solution)/shard_map/pallas_call | solution.py:527
  23.6 0.0 copy-done
  23.6 0.0 copy-done.1
  23.6 2.6 %shard_map.132 = (f32[5,125,512]{2,1,0:T(8,128)}, f32[5,125,512]{2,1,0:T(8,128)}) custom-call(f32[48,125,512]{2,1,0:T(8,128)} %shard_map.131.stored_in, f32[5,125,512]{2,1,0:T(8,128)S(1)} %copy-done, f32[5,125,512]{2,1,0:T(8,128)S(1)} %copy-done.1), custom_call_target="tpu_custom_call" | custom-call | tf_op jit(solution)/shard_map/pallas_call | solution.py:569
Async XLA Ops:
  0.6 23.0 %copy-start = (f32[5,125,512]{2,1,0:T(8,128)S(1)}, f32[5,125,512]{2,1,0:T(8,128)}, u32[]{:S(2)}) copy-start(f32[5,125,512]{2,1,0:T(8,128)} %fields.1) | copy-start | bytes 3840004
  0.6 23.0 %copy-start.1 = (f32[5,125,512]{2,1,0:T(8,128)S(1)}, f32[5,125,512]{2,1,0:T(8,128)}, u32[]{:S(2)}) copy-start(f32[5,125,512]{2,1,0:T(8,128)} %store.1) | copy-start | bytes 3840004
